TPU v7x, 512 devices: a whole 4x4x16 slice. The times are simulated.
512 devices in a mesh: section: 8 (over x, y_hi), expert: 16 (over z), shard: 4 (over y_lo, core).
Axes of the slice: x: 4, y: 4 (y_hi: 2, y_lo: 2; y = y_hi * 2 + y_lo), z: 16, core: 2. Of those that a mesh axis runs over, the one named last changes fastest.
Arguments:
- fwd_in: bfloat16 [8, 2048, 3584], P('section', 'expert', 'shard'), may hold values from -6 to 6
- saved_in: bfloat16 [8, 2048, 3584], P('section', 'expert', 'shard'), may hold values from -6 to 6
- grad_in: bfloat16 [8, 2048, 3584], P('section', 'expert', 'shard'), may hold values from -6 to 6
- w_in: bfloat16 [8, 16, 3584, 1024], P('section', 'expert', 'shard'), may hold values from -0.09375 to 0.09375
- w_out: bfloat16 [8, 16, 1024, 3584], P('section', 'expert', None, 'shard'), may hold values from -0.1875 to 0.1875
- ids_fwd: int32 [8, 2048, 2], P('section', 'expert'), may hold values from 0 to 15, all different within a row; in each aligned block of 128 rows (0 to 127, 128 to 255, ..., all dimensions but the last counted through in order) at most 20 rows name the same one
- weight_fwd: int32 [8, 2048, 2], P('section', 'expert'), may hold values from 3277 to 65535
- ids_bwd: int32 [8, 2048, 2], P('section', 'expert'), may hold values from 0 to 15, all different within a row; in each aligned block of 128 rows (0 to 127, 128 to 255, ..., all dimensions but the last counted through in order) at most 20 rows name the same one
- weight_bwd: int32 [8, 2048, 2], P('section', 'expert'), may hold values from 3277 to 65535
Outputs:
- fwd_out: bfloat16 [8, 2048, 3584], P('section', 'expert', 'shard')
- bwd_out: bfloat16 [8, 2048, 3584], P('section', 'expert', 'shard')
Inputs may be any that keep to these rules, and one draw needn't show every extreme that they name: `ids_fwd`: the 2 experts of a token differ. In each layer, among the 128 tokens of one index of the expert axis, no expert is chosen by more than 20 slots. `ids_bwd`: the 2 experts of a token differ. In each layer, among the 128 tokens of one index of the expert axis, no expert is chosen by more than 20 slots.
All inputs are finite; a program needn't handle non-finite values.
Results may differ from a plain program's by a relative error of at most 0.0049.
Values may be sent and summed in bfloat16 or wider, within the bound.
No kernel may reach another device: no remote copies, remote signals or barrier semaphores. Data moves between devices by JAX's collectives and lax.ppermute only.
A program may use at most 64 MiB of HBM per device.

v0:
```python
import jax
import jax.numpy as jnp
from jax import lax
from jax.sharding import PartitionSpec as P


def sent_together(arrays, axis, split_dim, concat_dim, along):
    widths = [a.shape[along] for a in arrays]
    both = jnp.concatenate(arrays, axis=along)
    filled = lax.all_to_all(both, axis, split_axis=split_dim, concat_axis=concat_dim, tiled=True)
    return tuple(jnp.split(filled, [sum(widths[:k]) for k in range(1, len(widths))], axis=along))


def cut_along(array, dim, peers):
    lengths = array.shape
    tiles = array.reshape(*lengths[:dim], peers, lengths[dim] // peers, *lengths[dim + 1 :])
    return jnp.moveaxis(tiles, dim, 0)


def summed_on_arrival(array, axis, dim):
    tiles = cut_along(array, dim, lax.axis_size(axis))
    arrived = lax.all_to_all(tiles, axis, split_axis=0, concat_axis=0, tiled=True)
    return arrived.sum(axis=0)


def from_behind(value, axis, steps):
    count = lax.axis_size(axis)
    pairs = [(source, (source + steps) % count) for source in range(count)]
    return lax.ppermute(value, axis, pairs)


def in_one_piece(arrays, axis, dim, along):
    widths = [a.shape[along] for a in arrays]
    both = jnp.concatenate(arrays, axis=along)
    filled = summed_on_arrival(both, axis, dim)
    return tuple(jnp.split(filled, [sum(widths[:k]) for k in range(1, len(widths))], axis=along))


def destinations(route_ids, experts, capacity):
    tokens, slot_count = route_ids.shape
    flat_ids = route_ids.reshape(-1)
    labels = jnp.arange(experts, dtype=jnp.int32)
    onehot = (flat_ids[:, None] == labels[None, :]).astype(jnp.int32)
    before = jnp.cumsum(onehot, axis=0) - onehot
    ranking = jnp.sum(before * onehot, axis=1)
    return (flat_ids * capacity + ranking).reshape(tokens, slot_count)


def dispatch_matrix(targets, slot_total):
    labels = jnp.arange(slot_total, dtype=jnp.int32)
    hits = jnp.zeros((slot_total, targets.shape[0]), jnp.float32)
    for column in range(targets.shape[1]):
        hits = hits + (labels[:, None] == targets[None, :, column]).astype(jnp.float32)
    return hits.astype(jnp.bfloat16)


def by_expert(received, expert_group, local_experts, capacity):
    features = received.shape[-1]
    shaped = received.reshape(expert_group, local_experts, capacity, features)
    return shaped.transpose(1, 0, 2, 3).reshape(local_experts, expert_group * capacity, features)


def by_source(results, expert_group, local_experts, capacity):
    features = results.shape[-1]
    shaped = results.reshape(local_experts, expert_group, capacity, features)
    return shaped.transpose(1, 0, 2, 3).reshape(expert_group * local_experts * capacity, features)


def mix_rows(tok_rows, targets, route_weight, returned):
    picked = returned[targets].astype(jnp.float32)
    slot_weight = route_weight.astype(jnp.float32) / 32768.0
    summed = jnp.sum(slot_weight[:, :, None] * picked, axis=1)
    return (tok_rows.astype(jnp.float32) + summed).astype(jnp.bfloat16)


def per_device(fwd_in, saved_in, grad_in, w_in, w_out, ids_fwd, weight_fwd, ids_bwd, weight_bwd):
    expert_group = lax.axis_size("expert")
    local_experts = w_in.shape[1]
    experts = expert_group * local_experts
    tok_count = fwd_in.shape[1]
    slot_count = ids_fwd.shape[2]
    capacity = max(2, (tok_count * slot_count * 5 + 4 * experts - 1) // (4 * experts))
    slot_total = experts * capacity
    up_local = w_in[0]
    down_local = w_out[0]
    fwd_rows = fwd_in[0]
    saved_rows = saved_in[0]
    grad_rows = grad_in[0]
    fwd_targets = destinations(ids_fwd[0], experts, capacity)
    fwd_picker = dispatch_matrix(fwd_targets, slot_total)
    fwd_packed = jnp.dot(fwd_picker, fwd_rows, preferred_element_type=jnp.float32).astype(
        jnp.bfloat16
    )
    fwd_received = lax.all_to_all(fwd_packed, "expert", split_axis=0, concat_axis=0, tiled=True)
    fwd_slots = by_expert(fwd_received, expert_group, local_experts, capacity)
    bwd_targets = destinations(ids_bwd[0], experts, capacity)
    bwd_picker = dispatch_matrix(bwd_targets, slot_total)
    bwd_packed = jnp.dot(bwd_picker, saved_rows, preferred_element_type=jnp.float32).astype(
        jnp.bfloat16
    )
    grad_packed = jnp.dot(bwd_picker, grad_rows, preferred_element_type=jnp.float32).astype(
        jnp.bfloat16
    )
    bwd_received, grad_received = sent_together((bwd_packed, grad_packed), "expert", 0, 0, 1)
    bwd_slots = by_expert(bwd_received, expert_group, local_experts, capacity)
    grad_slots = by_expert(grad_received, expert_group, local_experts, capacity)
    partial_value = jnp.einsum(
        "erd,edf->erf", fwd_slots, up_local, preferred_element_type=jnp.float32
    )
    hidden = summed_on_arrival(partial_value, "shard", 2)
    active_part = jax.nn.silu(hidden).astype(jnp.bfloat16)
    active = lax.all_gather(active_part, "shard", axis=2, tiled=True)
    fwd_results = jnp.einsum(
        "erf,efd->erd", active, down_local, preferred_element_type=jnp.float32
    ).astype(jnp.bfloat16)
    fwd_returned = lax.all_to_all(
        by_source(fwd_results, expert_group, local_experts, capacity),
        "expert",
        split_axis=0,
        concat_axis=0,
        tiled=True,
    )
    layer_out = mix_rows(fwd_rows, fwd_targets, weight_fwd[0], fwd_returned)
    fwd_out = from_behind(layer_out, "section", 1)
    partial_hidden = jnp.einsum(
        "erd,edf->erf", bwd_slots, up_local, preferred_element_type=jnp.float32
    )
    partial_slope = jnp.einsum(
        "erd,efd->erf", grad_slots, down_local, preferred_element_type=jnp.float32
    )
    back_hidden, slope_in = in_one_piece((partial_hidden, partial_slope), "shard", 2, 0)
    squash = jax.nn.sigmoid(back_hidden)
    slope_part = (slope_in * squash * (1.0 + back_hidden * (1.0 - squash))).astype(jnp.bfloat16)
    slope = lax.all_gather(slope_part, "shard", axis=2, tiled=True)
    bwd_results = jnp.einsum(
        "erf,edf->erd", slope, up_local, preferred_element_type=jnp.float32
    ).astype(jnp.bfloat16)
    bwd_returned = lax.all_to_all(
        by_source(bwd_results, expert_group, local_experts, capacity),
        "expert",
        split_axis=0,
        concat_axis=0,
        tiled=True,
    )
    layer_grad = mix_rows(grad_rows, bwd_targets, weight_bwd[0], bwd_returned)
    bwd_out = from_behind(layer_grad, "section", -1)
    return (fwd_out[None], bwd_out[None])


def solution(mesh):
    in_specs = (
        P("section", "expert", "shard"),
        P("section", "expert", "shard"),
        P("section", "expert", "shard"),
        P("section", "expert", "shard", None),
        P("section", "expert", None, "shard"),
        P("section", "expert", None),
        P("section", "expert", None),
        P("section", "expert", None),
        P("section", "expert", None),
    )
    out_specs = (P("section", "expert", "shard"), P("section", "expert", "shard"))
    return jax.shard_map(
        per_device, mesh=mesh, in_specs=in_specs, out_specs=out_specs, check_vma=False
    )
```

profile of v0, /device:TPU:54, one launch (start us, length us, event | category | flops | bytes accessed | tf_op | source)
XLA Modules:
  0.0 295.4 jit_solution(17760032897972907076)
XLA Ops:
  5.4 15.2 %all-to-all-start = ((bf16[16,20,896]{2,1,0:T(8,128)(2,1)}), bf16[16,20,896]{2,1,0:T(8,128)(2,1)}, u32[]{:S(2)}, u32[]{:S(2)}) async-start(bf16[16,20,896]{2,1,0:T(8,128)(2,1)} %all_to_all.36), calls=%async_computation | async-start | bytes 1376256 | tf_op jit(solution)/shard_map/all_to_all | solution.py:94
  24.2 31.7 %all-to-all-done = bf16[16,20,896]{2,1,0:T(8,128)(2,1)} async-done(((bf16[16,20,896]{2,1,0:T(8,128)(2,1)}), bf16[16,20,896]{2,1,0:T(8,128)(2,1)}, u32[]{:S(2)}, u32[]{:S(2)}) %all-to-all-start) | async-done | bytes 573472 | tf_op jit(solution)/shard_map/all_to_all | solution.py:94
  55.9 7.2 %all-to-all-start.3 = ((bf16[16,20,1792]{2,1,0:T(8,128)(2,1)}), bf16[16,20,1792]{2,1,0:T(8,128)(2,1)S(1)}, u32[]{:S(2)}, u32[]{:S(2)}) async-start(bf16[16,20,1792]{2,1,0:T(8,128)(2,1)} %all_to_all.42), calls=%async_computation.3 | async-start | bytes 2752512 | tf_op jit(solution)/shard_map/all_to_all | solution.py:10
  63.1 3.8 %copy.53 = bf16[1024,896]{1,0:T(8,128)(2,1)} copy(bf16[1024,896]{0,1:T(8,128)(2,1)} %bitcast.127) | data formatting | bytes 3670016 | tf_op jit(solution)/shard_map/erd,edf->erf/dot_general | solution.py:107
  66.9 2.0 reshape.261
  68.9 3.6 %convolution_bitcast_fusion.2 = f32[4,1,320,256]{3,2,1,0:T(8,128)} fusion(bf16[320,896,1]{1,0,2:T(8,128)(2,1)} %reshape.261, bf16[4,256,896]{2,1,0:T(8,128)(2,1)} %bitcast.128), kind=kOutput, calls=%fused_computation.9 | convolution fusion | flops 587202560 | bytes 3719168 | tf_op jit(solution)/shard_map/erd,edf->erf/dot_general | solution.py:107
  72.6 55.1 %all-to-all-done.3 = bf16[16,20,1792]{2,1,0:T(8,128)(2,1)S(1)} async-done(((bf16[16,20,1792]{2,1,0:T(8,128)(2,1)}), bf16[16,20,1792]{2,1,0:T(8,128)(2,1)S(1)}, u32[]{:S(2)}, u32[]{:S(2)}) %all-to-all-start.3) | async-done | bytes 1146912 | tf_op jit(solution)/shard_map/all_to_all | solution.py:10
  127.7 4.3 %all-to-all-start.1 = ((f32[4,1,320,256]{3,2,1,0:T(8,128)}), f32[4,1,320,256]{3,2,1,0:T(8,128)}, u32[]{:S(2)}, u32[]{:S(2)}) async-start(f32[4,1,320,256]{3,2,1,0:T(8,128)} %convolution_bitcast_fusion.2), calls=%async_computation.1 | async-start | bytes 2621440 | tf_op jit(solution)/shard_map/all_to_all | solution.py:22
  133.2 2.6 convolution_bitcast_fusion.1
  138.7 10.6 %all-to-all-done.1 = f32[4,1,320,256]{3,2,1,0:T(8,128)} async-done(((f32[4,1,320,256]{3,2,1,0:T(8,128)}), f32[4,1,320,256]{3,2,1,0:T(8,128)}, u32[]{:S(2)}, u32[]{:S(2)}) %all-to-all-start.1) | async-done | bytes 1310752 | tf_op jit(solution)/shard_map/all_to_all | solution.py:22
  149.3 4.6 %all-to-all-start.4 = ((f32[4,2,320,256]{3,2,1,0:T(8,128)}), f32[4,2,320,256]{3,2,1,0:T(8,128)}, u32[]{:S(2)}, u32[]{:S(2)}) async-start(f32[4,2,320,256]{3,2,1,0:T(8,128)} %copy.52), calls=%async_computation.4 | async-start | bytes 5242880 | tf_op jit(solution)/shard_map/all_to_all | solution.py:22
  155.4 34.1 %all_gather.6 = bf16[1,320,1024]{2,1,0:T(8,128)(2,1)S(1)} all-gather(bf16[1,320,256]{2,1,0:T(8,128)(2,1)S(1)} %fusion.17), channel_id=1, replica_groups=mesh['section'=8,'expert'=16,'shard'=4] {'shard'}, dimensions={2}, use_global_device_ids=true | all-gather | bytes 819200 | tf_op jit(solution)/shard_map/all_gather | solution.py:112
  191.3 7.4 %all-to-all-start.2 = ((bf16[16,20,896]{2,1,0:T(8,128)(2,1)}), bf16[16,20,896]{2,1,0:T(8,128)(2,1)S(1)}, u32[]{:S(2)}, u32[]{:S(2)}) async-start(bf16[16,20,896]{2,1,0:T(8,128)(2,1)} %all_to_all.39), calls=%async_computation.2 | async-start | bytes 1376256 | tf_op jit(solution)/shard_map/all_to_all | solution.py:116
  198.7 2.0 reduce_sum.72
  200.9 7.4 %all_gather.7 = bf16[1,320,1024]{2,1,0:T(8,128)(2,1)S(1)} all-gather(bf16[1,320,256]{2,1,0:T(8,128)(2,1)S(1)} %fusion.13), channel_id=1, replica_groups=mesh['section'=8,'expert'=16,'shard'=4] {'shard'}, dimensions={2}, use_global_device_ids=true | all-gather | bytes 819200 | tf_op jit(solution)/shard_map/all_gather | solution.py:134
  208.3 3.2 %fusion.4 = bf16[320,896]{1,0:T(8,128)(2,1)} fusion(bf16[1,1,896,1024]{3,2,1,0:T(8,128)(2,1)} %param.12, bf16[1,320,1024]{2,1,0:T(8,128)(2,1)S(1)} %all_gather.7), kind=kOutput, calls=%fused_computation.10 | convolution fusion | flops 587489280 | bytes 3063808 | tf_op jit(solution)/shard_map/erf,edf->erd/dot_general | solution.py:135
  211.5 2.0 all_to_all.46
  213.5 20.9 %all-to-all-done.2 = bf16[16,20,896]{2,1,0:T(8,128)(2,1)S(1)} async-done(((bf16[16,20,896]{2,1,0:T(8,128)(2,1)}), bf16[16,20,896]{2,1,0:T(8,128)(2,1)S(1)}, u32[]{:S(2)}, u32[]{:S(2)}) %all-to-all-start.2) | async-done | bytes 573472 | tf_op jit(solution)/shard_map/all_to_all | solution.py:116
  234.5 7.2 %all-to-all-start.5 = ((bf16[16,20,896]{2,1,0:T(8,128)(2,1)}), bf16[16,20,896]{2,1,0:T(8,128)(2,1)}, u32[]{:S(2)}, u32[]{:S(2)}) async-start(bf16[16,20,896]{2,1,0:T(8,128)(2,1)} %all_to_all.46), calls=%async_computation.5 | async-start | bytes 1376256 | tf_op jit(solution)/shard_map/all_to_all | solution.py:138
  246.9 2.0 multiply_reduce_fusion.1
  249.7 2.1 collective-permute-start
  251.8 25.5 %all-to-all-done.5 = bf16[16,20,896]{2,1,0:T(8,128)(2,1)} async-done(((bf16[16,20,896]{2,1,0:T(8,128)(2,1)}), bf16[16,20,896]{2,1,0:T(8,128)(2,1)}, u32[]{:S(2)}, u32[]{:S(2)}) %all-to-all-start.5) | async-done | bytes 573472 | tf_op jit(solution)/shard_map/all_to_all | solution.py:138
  281.5 2.2 collective-permute-start.1
  283.8 9.3 %collective-permute-done.1 = bf16[128,896]{1,0:T(8,128)(2,1)S(1)} collective-permute-done((bf16[128,896]{1,0:T(8,128)(2,1)S(1)}, bf16[128,896]{1,0:T(8,128)(2,1)S(1)}, u32[]{:S(2)}, u32[]{:S(2)}) %collective-permute-start.1) | collective-permute-done | bytes 229408 | tf_op jit(solution)/shard_map/ppermute | solution.py:29
  (86 shorter events, 28.0 us)
Async XLA Ops:
  0.6 135.2 %copy-start = (bf16[1,1,1024,896]{3,2,1,0:T(8,128)(2,1)S(1)}, bf16[1,1,1024,896]{3,2,1,0:T(8,128)(2,1)}, u32[]{:S(2)}) copy-start(bf16[1,1,1024,896]{3,2,1,0:T(8,128)(2,1)} %param.13) | copy-start | bytes 5505028
  2.9 17.6 %copy-start.8 = (s32[1,128,2]{1,2,0:T(2,128)S(1)}, s32[1,128,2]{1,2,0:T(2,128)}, u32[]{:S(2)}) copy-start(s32[1,128,2]{1,2,0:T(2,128)} %param.16) | copy-start | bytes 3076
  4.4 17.9 %copy-start.4 = (bf16[1,128,896]{2,1,0:T(8,128)(2,1)S(1)}, bf16[1,128,896]{2,1,0:T(8,128)(2,1)}, u32[]{:S(2)}) copy-start(bf16[1,128,896]{2,1,0:T(8,128)(2,1)} %param.11) | copy-start | bytes 688132
  4.4 18.2 %copy-start.7 = (bf16[1,128,896]{2,1,0:T(8,128)(2,1)S(1)}, bf16[1,128,896]{2,1,0:T(8,128)(2,1)}, u32[]{:S(2)}) copy-start(bf16[1,128,896]{2,1,0:T(8,128)(2,1)} %param.10) | copy-start | bytes 688132
  5.4 50.5 %all-to-all-start = ((bf16[16,20,896]{2,1,0:T(8,128)(2,1)}), bf16[16,20,896]{2,1,0:T(8,128)(2,1)}, u32[]{:S(2)}, u32[]{:S(2)}) async-start(bf16[16,20,896]{2,1,0:T(8,128)(2,1)} %all_to_all.36), calls=%async_computation | async-start | bytes 1376256 | tf_op jit(solution)/shard_map/all_to_all | solution.py:94
  55.9 71.8 %all-to-all-start.3 = ((bf16[16,20,1792]{2,1,0:T(8,128)(2,1)}), bf16[16,20,1792]{2,1,0:T(8,128)(2,1)S(1)}, u32[]{:S(2)}, u32[]{:S(2)}) async-start(bf16[16,20,1792]{2,1,0:T(8,128)(2,1)} %all_to_all.42), calls=%async_computation.3 | async-start | bytes 2752512 | tf_op jit(solution)/shard_map/all_to_all | solution.py:10
  127.7 21.6 %all-to-all-start.1 = ((f32[4,1,320,256]{3,2,1,0:T(8,128)}), f32[4,1,320,256]{3,2,1,0:T(8,128)}, u32[]{:S(2)}, u32[]{:S(2)}) async-start(f32[4,1,320,256]{3,2,1,0:T(8,128)} %convolution_bitcast_fusion.2), calls=%async_computation.1 | async-start | bytes 2621440 | tf_op jit(solution)/shard_map/all_to_all | solution.py:22
  133.2 2.7 copy-start.2
  149.3 42.0 %all-to-all-start.4 = ((f32[4,2,320,256]{3,2,1,0:T(8,128)}), f32[4,2,320,256]{3,2,1,0:T(8,128)}, u32[]{:S(2)}, u32[]{:S(2)}) async-start(f32[4,2,320,256]{3,2,1,0:T(8,128)} %copy.52), calls=%async_computation.4 | async-start | bytes 5242880 | tf_op jit(solution)/shard_map/all_to_all | solution.py:22
  191.3 43.1 %all-to-all-start.2 = ((bf16[16,20,896]{2,1,0:T(8,128)(2,1)}), bf16[16,20,896]{2,1,0:T(8,128)(2,1)S(1)}, u32[]{:S(2)}, u32[]{:S(2)}) async-start(bf16[16,20,896]{2,1,0:T(8,128)(2,1)} %all_to_all.39), calls=%async_computation.2 | async-start | bytes 1376256 | tf_op jit(solution)/shard_map/all_to_all | solution.py:116
  211.5 30.6 %copy-start.9 = (s32[1,128,2]{1,2,0:T(2,128)S(1)}, s32[1,128,2]{1,2,0:T(2,128)}, u32[]{:S(2)}) copy-start(s32[1,128,2]{1,2,0:T(2,128)} %param.15) | copy-start | bytes 3076
  211.5 31.5 %copy-start.10 = (s32[1,128,2]{1,2,0:T(2,128)S(1)}, s32[1,128,2]{1,2,0:T(2,128)}, u32[]{:S(2)}) copy-start(s32[1,128,2]{1,2,0:T(2,128)} %param.17) | copy-start | bytes 3076
  234.5 42.9 %all-to-all-start.5 = ((bf16[16,20,896]{2,1,0:T(8,128)(2,1)}), bf16[16,20,896]{2,1,0:T(8,128)(2,1)}, u32[]{:S(2)}, u32[]{:S(2)}) async-start(bf16[16,20,896]{2,1,0:T(8,128)(2,1)} %all_to_all.46), calls=%async_computation.5 | async-start | bytes 1376256 | tf_op jit(solution)/shard_map/all_to_all | solution.py:138
  246.4 2.5 copy-start.3
  246.9 31.7 %copy-start.1 = (s32[1024]{0:T(1024)S(1)}, s32[1024]{0:T(1024)}, u32[]{:S(2)}) copy-start(s32[1024]{0:T(1024)} %pad_clamp_fusion) | copy-start | bytes 12292
  249.7 34.1 %collective-permute-start = (bf16[128,896]{1,0:T(8,128)(2,1)}, bf16[128,896]{1,0:T(8,128)(2,1)}, u32[]{:S(2)}, u32[]{:S(2)}) collective-permute-start(bf16[128,896]{1,0:T(8,128)(2,1)} %add_convert_fusion.1), channel_id=1, source_target_pairs={{0,64},{64,128},{128,192},{192,256},{256,320},{320,384},{384,448},... | collective-permute-start | bytes 688136 | tf_op jit(solution)/shard_map/ppermute | solution.py:29
  278.6 1.7 copy-start.6
  279.8 1.6 copy-start.5
  281.5 11.5 %collective-permute-start.1 = (bf16[128,896]{1,0:T(8,128)(2,1)S(1)}, bf16[128,896]{1,0:T(8,128)(2,1)S(1)}, u32[]{:S(2)}, u32[]{:S(2)}) collective-permute-start(bf16[128,896]{1,0:T(8,128)(2,1)S(1)} %add_convert_fusion), channel_id=1, source_target_pairs={{0,448},{64,0},{128,64},{192,128},{256,192},{320,256},{384,320},{4... | collective-permute-start | bytes 688136 | tf_op jit(solution)/shard_map/ppermute | solution.py:29
where the time goes:
time: 296 us; the launch traced here: 295 us
  waiting for transfers between devices  153 us (52%)
  starting transfers between devices  50.3 us (17%)
  blocking collectives  41.5 us (14%)
  local copies, waits for them, and re-layouts  25.8 us (9%)
  matrix products  13 us (4%)
  other arithmetic  10.6 us (4%)
    all_to_all x1, waiting for transfers between devices, sent_together(): lax.all_to_all(both, axis, split_axis=split_dim, concat_axis=concat_dim,...  55.1 us
    all_gather x1, blocking collectives, per_device(): active = lax.all_gather(active_part, 'shard', axis=2, tiled=True)  34.1 us
    all_to_all x1, waiting for transfers between devices, per_device(): lax.all_to_all(fwd_packed, 'expert', split_axis=0, concat_axis=0, tiled=T...  31.7 us
    all_to_all x1, waiting for transfers between devices, per_device(): lax.all_to_all(by_source(bwd_results, expert_group, local_experts, capaci...  25.5 us
    all_to_all x1, waiting for transfers between devices, per_device(): lax.all_to_all(by_source(fwd_results, expert_group, local_experts, capaci...  20.9 us
    all_to_all x1, starting transfers between devices, per_device(): lax.all_to_all(fwd_packed, 'expert', split_axis=0, concat_axis=0, tiled=T...  15.2 us
    all_to_all x2, waiting for transfers between devices, summed_on_arrival(): lax.all_to_all(tiles, axis, split_axis=0, concat_axis=0, tiled=True)  10.6 us
    ppermute x2, waiting for transfers between devices, from_behind(): return lax.ppermute(value, axis, pairs)  9.27 us
  transfers between devices with their start and end apart: 8, of which 6 were waited for; matrix products, arithmetic and copies ran while one was open for 12% of the time, Pallas kernels for 0%

commit v1 on v0

--- a/solution.py
+++ b/solution.py
@@ -109,7 +109,9 @@
     )
     hidden = summed_on_arrival(partial_value, "shard", 2)
     active_part = jax.nn.silu(hidden).astype(jnp.bfloat16)
-    active = lax.all_gather(active_part, "shard", axis=2, tiled=True)
+    active = jnp.concatenate(
+        lax.all_to_all(jnp.stack([active_part] * lax.axis_size("shard")), "shard", 0, 0), axis=2
+    )
     fwd_results = jnp.einsum(
         "erf,efd->erd", active, down_local, preferred_element_type=jnp.float32
     ).astype(jnp.bfloat16)

time: 296 us -> 308 us (1.041)
  waiting for transfers between devices: 153 us -> 189 us
  blocking collectives: 41.5 us -> 6.86 us
  starting transfers between devices: 50.3 us -> 54.5 us
  other arithmetic: 10.6 us -> 14 us
    all_gather x1 -> x0, blocking collectives: 34.1 us -> none  [per_device(): active = lax.all_gather(active_part, 'shard', axis=2, tiled=True)]
    all_to_all x2, waiting for transfers between devices: 10.6 us -> 38.9 us  [summed_on_arrival(): lax.all_to_all(tiles, axis, split_axis=0, concat_axis=0, tiled=True)]
    all_to_all x1, waiting for transfers between devices: 55.1 us -> 60.3 us  [sent_together(): lax.all_to_all(both, axis, split_axis=split_dim, concat_axis=concat_dim,...]
    all_to_all x0 -> x1, starting transfers between devices: none -> 4.15 us  [per_device(): lax.all_to_all(jnp.stack([active_part] * lax.axis_size('shard')), 'shard'...]
    all_to_all x0 -> x1, waiting for transfers between devices: none -> 3.58 us  [per_device(): lax.all_to_all(jnp.stack([active_part] * lax.axis_size('shard')), 'shard'...]
  transfers between devices with their start and end apart: 8 -> 9, of which waited for: 6 -> 8; matrix products, arithmetic and copies ran while one was open for 12% -> 12% of each run, Pallas kernels for 0% -> 0%
where the time goes in v1:
time: 308 us; the launch traced here: 306 us
  waiting for transfers between devices  189 us (61%)
  starting transfers between devices  54.5 us (18%)
  local copies, waits for them, and re-layouts  26.8 us (9%)
  other arithmetic  14 us (5%)
  matrix products  13.9 us (5%)
  blocking collectives  6.86 us (2%)
    all_to_all x1, waiting for transfers between devices, sent_together(): lax.all_to_all(both, axis, split_axis=split_dim, concat_axis=concat_dim,...  60.3 us
    all_to_all x2, waiting for transfers between devices, summed_on_arrival(): lax.all_to_all(tiles, axis, split_axis=0, concat_axis=0, tiled=True)  38.9 us
    all_to_all x1, waiting for transfers between devices, per_device(): lax.all_to_all(fwd_packed, 'expert', split_axis=0, concat_axis=0, tiled=T...  29.9 us
    all_to_all x1, waiting for transfers between devices, per_device(): lax.all_to_all(by_source(bwd_results, expert_group, local_experts, capaci...  26.9 us
    all_to_all x1, waiting for transfers between devices, per_device(): lax.all_to_all(by_source(fwd_results, expert_group, local_experts, capaci...  20.5 us
    all_to_all x1, starting transfers between devices, per_device(): lax.all_to_all(fwd_packed, 'expert', split_axis=0, concat_axis=0, tiled=T...  15.2 us
    ppermute x2, waiting for transfers between devices, from_behind(): return lax.ppermute(value, axis, pairs)  9.27 us
    all_to_all x2, starting transfers between devices, summed_on_arrival(): lax.all_to_all(tiles, axis, split_axis=0, concat_axis=0, tiled=True)  8.08 us
  transfers between devices with their start and end apart: 9, of which 8 were waited for; matrix products, arithmetic and copies ran while one was open for 12% of the time, Pallas kernels for 0%

profile of v1, /device:TPU:54, one launch (start us, length us, event | category | flops | bytes accessed | tf_op | source)
XLA Modules:
  0.0 306.5 jit_solution(643702351757878428)
XLA Ops:
  5.3 15.2 %all-to-all-start = ((bf16[16,20,896]{2,1,0:T(8,128)(2,1)}), bf16[16,20,896]{2,1,0:T(8,128)(2,1)S(1)}, u32[]{:S(2)}, u32[]{:S(2)}) async-start(bf16[16,20,896]{2,1,0:T(8,128)(2,1)} %all_to_all.39), calls=%async_computation | async-start | bytes 1376256 | tf_op jit(solution)/shard_map/all_to_all | solution.py:94
  21.0 3.8 %copy.54 = bf16[1024,896]{1,0:T(8,128)(2,1)} copy(bf16[1024,896]{0,1:T(8,128)(2,1)} %bitcast.117) | data formatting | bytes 3670016 | tf_op jit(solution)/shard_map/erd,edf->erf/dot_general | solution.py:107
  25.9 29.9 %all-to-all-done = bf16[16,20,896]{2,1,0:T(8,128)(2,1)S(1)} async-done(((bf16[16,20,896]{2,1,0:T(8,128)(2,1)}), bf16[16,20,896]{2,1,0:T(8,128)(2,1)S(1)}, u32[]{:S(2)}, u32[]{:S(2)}) %all-to-all-start) | async-done | bytes 573472 | tf_op jit(solution)/shard_map/all_to_all | solution.py:94
  55.9 3.4 %convolution_bitcast_fusion.2 = f32[4,1,320,256]{3,2,1,0:T(8,128)} fusion(bf16[320,896,1]{1,0,2:T(8,128)(2,1)S(1)} %reshape.256, bf16[4,256,896]{2,1,0:T(8,128)(2,1)} %bitcast.118), kind=kOutput, calls=%fused_computation.9 | convolution fusion | flops 587202560 | bytes 3719168 | tf_op jit(solution)/shard_map/erd,edf->erf/dot_general | solution.py:107
  59.3 3.5 %all-to-all-start.1 = ((f32[4,1,320,256]{3,2,1,0:T(8,128)}), f32[4,1,320,256]{3,2,1,0:T(8,128)S(1)}, u32[]{:S(2)}, u32[]{:S(2)}) async-start(f32[4,1,320,256]{3,2,1,0:T(8,128)} %convolution_bitcast_fusion.2), calls=%async_computation.1 | async-start | bytes 2621440 | tf_op jit(solution)/shard_map/all_to_all | solution.py:22
  66.7 2.3 all_to_all.46
  68.9 11.1 %all-to-all-done.1 = f32[4,1,320,256]{3,2,1,0:T(8,128)S(1)} async-done(((f32[4,1,320,256]{3,2,1,0:T(8,128)}), f32[4,1,320,256]{3,2,1,0:T(8,128)S(1)}, u32[]{:S(2)}, u32[]{:S(2)}) %all-to-all-start.1) | async-done | bytes 1310752 | tf_op jit(solution)/shard_map/all_to_all | solution.py:22
  81.1 7.2 %all-to-all-start.4 = ((bf16[16,20,1792]{2,1,0:T(8,128)(2,1)}), bf16[16,20,1792]{2,1,0:T(8,128)(2,1)S(1)}, u32[]{:S(2)}, u32[]{:S(2)}) async-start(bf16[16,20,1792]{2,1,0:T(8,128)(2,1)} %all_to_all.46), calls=%async_computation.4 | async-start | bytes 2752512 | tf_op jit(solution)/shard_map/all_to_all | solution.py:10
  88.4 2.2 reduce_sum.64
  91.6 60.3 %all-to-all-done.4 = bf16[16,20,1792]{2,1,0:T(8,128)(2,1)S(1)} async-done(((bf16[16,20,1792]{2,1,0:T(8,128)(2,1)}), bf16[16,20,1792]{2,1,0:T(8,128)(2,1)S(1)}, u32[]{:S(2)}, u32[]{:S(2)}) %all-to-all-start.4) | async-done | bytes 1146912 | tf_op jit(solution)/shard_map/all_to_all | solution.py:10
  152.8 4.2 %all-to-all-start.2 = ((bf16[4,1,320,256]{3,2,1,0:T(8,128)(2,1)}), bf16[4,1,320,256]{3,2,1,0:T(8,128)(2,1)}, u32[]{:S(2)}, u32[]{:S(2)}) async-start(bf16[4,1,320,256]{3,2,1,0:T(8,128)(2,1)} %stack.2), calls=%async_computation.2 | async-start | bytes 1310720 | tf_op jit(solution)/shard_map/all_to_all | solution.py:113
  158.1 2.6 convolution_bitcast_fusion.1
  163.7 3.6 %all-to-all-done.2 = bf16[4,1,320,256]{3,2,1,0:T(8,128)(2,1)} async-done(((bf16[4,1,320,256]{3,2,1,0:T(8,128)(2,1)}), bf16[4,1,320,256]{3,2,1,0:T(8,128)(2,1)}, u32[]{:S(2)}, u32[]{:S(2)}) %all-to-all-start.2) | async-done | bytes 655392 | tf_op jit(solution)/shard_map/all_to_all | solution.py:113
  167.3 4.5 %all-to-all-start.5 = ((f32[4,2,320,256]{3,2,1,0:T(8,128)}), f32[4,2,320,256]{3,2,1,0:T(8,128)}, u32[]{:S(2)}, u32[]{:S(2)}) async-start(f32[4,2,320,256]{3,2,1,0:T(8,128)} %copy.53), calls=%async_computation.5 | async-start | bytes 5242880 | tf_op jit(solution)/shard_map/all_to_all | solution.py:22
  175.4 27.8 %all-to-all-done.5 = f32[4,2,320,256]{3,2,1,0:T(8,128)} async-done(((f32[4,2,320,256]{3,2,1,0:T(8,128)}), f32[4,2,320,256]{3,2,1,0:T(8,128)}, u32[]{:S(2)}, u32[]{:S(2)}) %all-to-all-start.5) | async-done | bytes 2621472 | tf_op jit(solution)/shard_map/all_to_all | solution.py:22
  203.2 8.0 %all-to-all-start.3 = ((bf16[16,20,896]{2,1,0:T(8,128)(2,1)}), bf16[16,20,896]{2,1,0:T(8,128)(2,1)S(1)}, u32[]{:S(2)}, u32[]{:S(2)}) async-start(bf16[16,20,896]{2,1,0:T(8,128)(2,1)} %all_to_all.43), calls=%async_computation.3 | async-start | bytes 1376256 | tf_op jit(solution)/shard_map/all_to_all | solution.py:118
  211.2 2.8 reduce_sum.69
  215.2 6.9 %all_gather.3 = bf16[1,320,1024]{2,1,0:T(8,128)(2,1)S(1)} all-gather(bf16[1,320,256]{2,1,0:T(8,128)(2,1)S(1)} %fusion.12), channel_id=1, replica_groups=mesh['section'=8,'expert'=16,'shard'=4] {'shard'}, dimensions={2}, use_global_device_ids=true | all-gather | bytes 819200 | tf_op jit(solution)/shard_map/all_gather | solution.py:136
  222.1 2.4 fusion.4
  225.5 20.5 %all-to-all-done.3 = bf16[16,20,896]{2,1,0:T(8,128)(2,1)S(1)} async-done(((bf16[16,20,896]{2,1,0:T(8,128)(2,1)}), bf16[16,20,896]{2,1,0:T(8,128)(2,1)S(1)}, u32[]{:S(2)}, u32[]{:S(2)}) %all-to-all-start.3) | async-done | bytes 573472 | tf_op jit(solution)/shard_map/all_to_all | solution.py:118
  246.0 7.4 %all-to-all-start.6 = ((bf16[16,20,896]{2,1,0:T(8,128)(2,1)}), bf16[16,20,896]{2,1,0:T(8,128)(2,1)}, u32[]{:S(2)}, u32[]{:S(2)}) async-start(bf16[16,20,896]{2,1,0:T(8,128)(2,1)} %all_to_all.50), calls=%async_computation.6 | async-start | bytes 1376256 | tf_op jit(solution)/shard_map/all_to_all | solution.py:140
  261.6 26.9 %all-to-all-done.6 = bf16[16,20,896]{2,1,0:T(8,128)(2,1)} async-done(((bf16[16,20,896]{2,1,0:T(8,128)(2,1)}), bf16[16,20,896]{2,1,0:T(8,128)(2,1)}, u32[]{:S(2)}, u32[]{:S(2)}) %all-to-all-start.6) | async-done | bytes 573472 | tf_op jit(solution)/shard_map/all_to_all | solution.py:140
  292.6 2.2 collective-permute-start.1
  294.9 9.3 %collective-permute-done.1 = bf16[128,896]{1,0:T(8,128)(2,1)S(1)} collective-permute-done((bf16[128,896]{1,0:T(8,128)(2,1)S(1)}, bf16[128,896]{1,0:T(8,128)(2,1)S(1)}, u32[]{:S(2)}, u32[]{:S(2)}) %collective-permute-start.1) | collective-permute-done | bytes 229408 | tf_op jit(solution)/shard_map/ppermute | solution.py:29
  (84 shorter events, 37.3 us)
Async XLA Ops:
  0.6 160.1 %copy-start = (bf16[1,1,1024,896]{3,2,1,0:T(8,128)(2,1)S(1)}, bf16[1,1,1024,896]{3,2,1,0:T(8,128)(2,1)}, u32[]{:S(2)}) copy-start(bf16[1,1,1024,896]{3,2,1,0:T(8,128)(2,1)} %param.13) | copy-start | bytes 5505028
  2.9 17.6 %copy-start.5 = (s32[1,128,2]{1,2,0:T(2,128)S(1)}, s32[1,128,2]{1,2,0:T(2,128)}, u32[]{:S(2)}) copy-start(s32[1,128,2]{1,2,0:T(2,128)} %param.16) | copy-start | bytes 3076
  5.3 50.4 %all-to-all-start = ((bf16[16,20,896]{2,1,0:T(8,128)(2,1)}), bf16[16,20,896]{2,1,0:T(8,128)(2,1)S(1)}, u32[]{:S(2)}, u32[]{:S(2)}) async-start(bf16[16,20,896]{2,1,0:T(8,128)(2,1)} %all_to_all.39), calls=%async_computation | async-start | bytes 1376256 | tf_op jit(solution)/shard_map/all_to_all | solution.py:94
  59.3 20.8 %all-to-all-start.1 = ((f32[4,1,320,256]{3,2,1,0:T(8,128)}), f32[4,1,320,256]{3,2,1,0:T(8,128)S(1)}, u32[]{:S(2)}, u32[]{:S(2)}) async-start(f32[4,1,320,256]{3,2,1,0:T(8,128)} %convolution_bitcast_fusion.2), calls=%async_computation.1 | async-start | bytes 2621440 | tf_op jit(solution)/shard_map/all_to_all | solution.py:22
  80.1 1.1 copy-start.1
  81.1 70.8 %all-to-all-start.4 = ((bf16[16,20,1792]{2,1,0:T(8,128)(2,1)}), bf16[16,20,1792]{2,1,0:T(8,128)(2,1)S(1)}, u32[]{:S(2)}, u32[]{:S(2)}) async-start(bf16[16,20,1792]{2,1,0:T(8,128)(2,1)} %all_to_all.46), calls=%async_computation.4 | async-start | bytes 2752512 | tf_op jit(solution)/shard_map/all_to_all | solution.py:10
  152.8 14.4 %all-to-all-start.2 = ((bf16[4,1,320,256]{3,2,1,0:T(8,128)(2,1)}), bf16[4,1,320,256]{3,2,1,0:T(8,128)(2,1)}, u32[]{:S(2)}, u32[]{:S(2)}) async-start(bf16[4,1,320,256]{3,2,1,0:T(8,128)(2,1)} %stack.2), calls=%async_computation.2 | async-start | bytes 1310720 | tf_op jit(solution)/shard_map/all_to_all | solution.py:113
  158.1 2.7 copy-start.2
  167.3 35.9 %all-to-all-start.5 = ((f32[4,2,320,256]{3,2,1,0:T(8,128)}), f32[4,2,320,256]{3,2,1,0:T(8,128)}, u32[]{:S(2)}, u32[]{:S(2)}) async-start(f32[4,2,320,256]{3,2,1,0:T(8,128)} %copy.53), calls=%async_computation.5 | async-start | bytes 5242880 | tf_op jit(solution)/shard_map/all_to_all | solution.py:22
  203.2 42.8 %all-to-all-start.3 = ((bf16[16,20,896]{2,1,0:T(8,128)(2,1)}), bf16[16,20,896]{2,1,0:T(8,128)(2,1)S(1)}, u32[]{:S(2)}, u32[]{:S(2)}) async-start(bf16[16,20,896]{2,1,0:T(8,128)(2,1)} %all_to_all.43), calls=%async_computation.3 | async-start | bytes 1376256 | tf_op jit(solution)/shard_map/all_to_all | solution.py:118
  224.5 29.3 %copy-start.6 = (s32[1,128,2]{1,2,0:T(2,128)S(1)}, s32[1,128,2]{1,2,0:T(2,128)}, u32[]{:S(2)}) copy-start(s32[1,128,2]{1,2,0:T(2,128)} %param.15) | copy-start | bytes 3076
  224.5 30.2 %copy-start.7 = (s32[1,128,2]{1,2,0:T(2,128)S(1)}, s32[1,128,2]{1,2,0:T(2,128)}, u32[]{:S(2)}) copy-start(s32[1,128,2]{1,2,0:T(2,128)} %param.17) | copy-start | bytes 3076
  246.0 42.5 %all-to-all-start.6 = ((bf16[16,20,896]{2,1,0:T(8,128)(2,1)}), bf16[16,20,896]{2,1,0:T(8,128)(2,1)}, u32[]{:S(2)}, u32[]{:S(2)}) async-start(bf16[16,20,896]{2,1,0:T(8,128)(2,1)} %all_to_all.50), calls=%async_computation.6 | async-start | bytes 1376256 | tf_op jit(solution)/shard_map/all_to_all | solution.py:140
  256.2 2.5 copy-start.3
  259.4 35.5 %collective-permute-start = (bf16[128,896]{1,0:T(8,128)(2,1)}, bf16[128,896]{1,0:T(8,128)(2,1)}, u32[]{:S(2)}, u32[]{:S(2)}) collective-permute-start(bf16[128,896]{1,0:T(8,128)(2,1)} %add_convert_fusion.1), channel_id=1, source_target_pairs={{0,64},{64,128},{128,192},{192,256},{256,320},{320,384},{384,448},... | collective-permute-start | bytes 688136 | tf_op jit(solution)/shard_map/ppermute | solution.py:29
  290.9 1.6 copy-start.4
  292.6 11.5 %collective-permute-start.1 = (bf16[128,896]{1,0:T(8,128)(2,1)S(1)}, bf16[128,896]{1,0:T(8,128)(2,1)S(1)}, u32[]{:S(2)}, u32[]{:S(2)}) collective-permute-start(bf16[128,896]{1,0:T(8,128)(2,1)S(1)} %add_convert_fusion), channel_id=1, source_target_pairs={{0,448},{64,0},{128,64},{192,128},{256,192},{320,256},{384,320},{4... | collective-permute-start | bytes 688136 | tf_op jit(solution)/shard_map/ppermute | solution.py:29
